TPU v7x, 32 devices: a whole 2x2x4 slice. The times are simulated.
32 devices in a mesh: row: 8 (over y, x, core), col: 4 (over z).
Axes of the slice: x: 2, y: 2, z: 4, core: 2. Of those that a mesh axis runs over, the one named last changes fastest.
Arguments:
- hidden_in: bfloat16 [1152, 2048], P('col', 'row'), may hold values from -21 to 21
- state: float32 [128, 2048, 1152], P('col', 'row'), may hold values from -4 to 4
- attn_norm_gain: bfloat16 [2048], replicated, may hold values from 0.099609375 to 1.8984375
- w_query: bfloat16 [2048, 2048], P(None, 'row'), may hold values from -0.125 to 0.125
- w_key: bfloat16 [2048, 2048], P(None, 'row'), may hold values from -0.125 to 0.125
- w_value: bfloat16 [2048, 2048], P(None, 'row'), may hold values from -0.125 to 0.125
- w_gate: bfloat16 [2048, 2048], P(None, 'row'), may hold values from -0.125 to 0.125
- w_decay: bfloat16 [2048, 16], replicated, may hold values from -0.125 to 0.125
- w_beta: bfloat16 [2048, 16], replicated, may hold values from -0.125 to 0.125
- decay_log: float32 [16], replicated, may hold values from -3 to 1.5
- decay_bias: float32 [16], replicated, may hold values from -2 to 1
- head_gain: float32 [128], replicated, may hold values from 0.1 to 1.9
- w_out: bfloat16 [2048, 2048], P('row'), may hold values from -0.125 to 0.125
- final_gain: bfloat16 [2048], P('row'), may hold values from 0.099609375 to 1.8984375
- lm_weight: bfloat16 [2048, 20480], P(None, ('row', 'col')), may hold values from -0.28726213 to 0.28726213
- token_ids: int32 [1152], replicated, may hold values from 0 to 20479
- ref_logprob: float32 [1152], replicated, may hold values from -16 to -6
Outputs:
- new_state: float32 [128, 2048, 1152], P('col', 'row')
- logprob: float32 [1152], replicated
- entropy: float32 [1152], replicated
- kl: float32 [1152], replicated
All inputs are finite; a program needn't handle non-finite values.
Results may differ from a plain program's by a relative error of at most 0.0014.
The roundings to bfloat16 on the way count: a program that leaves them out, or rounds other values in their place, can miss the bound.
Values may be sent and summed in bfloat16 or wider, within the bound.
A program may use at most 128 MiB of HBM per device.

v0:
```python
import jax
import jax.numpy as jnp
from jax import lax
from jax.sharding import PartitionSpec as P

D = 2048
HEADS = 16
DK = 128
DV = 128


def partner_2(block, axis, apart):
    count = lax.axis_size(axis)
    route = []
    for low in range(count):
        high = low | 1 << apart
        if high != low and high < count:
            route += [(low, high), (high, low)]
    return lax.ppermute(block, axis, route)


def project(weight, normed):
    return lax.dot_general(
        weight, normed, (((0,), (1,)), ((), ())), preferred_element_type=jnp.float32
    )


def shift_pairs(count, step):
    return [(source, (source + step) % count) for source in range(count)]


def swap_blocks(blocks, axis):
    count = lax.axis_size(axis)
    me = lax.axis_index(axis)
    result = blocks
    for step in range(1, count):
        sent = lax.dynamic_index_in_dim(blocks, (me + step) % count, 0, keepdims=True)
        got = lax.ppermute(sent, axis, shift_pairs(count, step))
        result = lax.dynamic_update_slice_in_dim(result, got, (me - step) % count, 0)
    return result


def gather_blocks(block, axis):
    count = lax.axis_size(axis)
    me = lax.axis_index(axis)
    result = jnp.zeros((count,) + block.shape, block.dtype)
    result = lax.dynamic_update_slice_in_dim(result, block[None], me, 0)
    for step in range(1, count):
        got = lax.ppermute(block[None], axis, shift_pairs(count, step))
        result = lax.dynamic_update_slice_in_dim(result, got, (me - step) % count, 0)
    return result


def sum_blocks(blocks, axis):
    count = lax.axis_size(axis)
    me = lax.axis_index(axis)
    total = lax.dynamic_index_in_dim(blocks, me, 0, keepdims=False)
    for step in range(1, count):
        sent = lax.dynamic_index_in_dim(blocks, (me + step) % count, 0, keepdims=False)
        total = total + lax.ppermute(sent, axis, shift_pairs(count, step))
    return total


def merge_stats(stats, axis):
    every = lax.all_gather(stats, axis, axis=0, tiled=False)
    top = jnp.max(every[:, 0], axis=0)
    shrink = jnp.exp(every[:, 0] - top[None])
    return jnp.stack(
        [
            top,
            jnp.sum(every[:, 1] * shrink, axis=0),
            jnp.sum(every[:, 2] * shrink, axis=0),
            jnp.sum(every[:, 3], axis=0),
        ]
    )


def per_device(
    hidden_in,
    state,
    attn_norm_gain,
    w_query,
    w_key,
    w_value,
    w_gate,
    w_decay,
    w_beta,
    decay_log,
    decay_bias,
    head_gain,
    w_out,
    final_gain,
    lm_weight,
    token_ids,
    ref_logprob,
):
    highest = lax.Precision.HIGHEST
    row_count = lax.axis_size("row")
    col_count = lax.axis_size("col")
    row_index = lax.axis_index("row")
    col_index = lax.axis_index("col")
    group = max(1, row_count // HEADS)
    local_heads = max(1, HEADS // row_count)
    first_head = row_index // group * local_heads
    value_cols = w_value.shape[1]
    value_part = value_cols // local_heads
    block_rows = hidden_in.shape[0]
    key_rows = state.shape[0]
    batch = state.shape[2]
    vocab_dev = lm_weight.shape[1]
    packed = jnp.concatenate([hidden_in, final_gain[None, :]], axis=0)
    whole = lax.all_gather(packed, "row", axis=1, tiled=True)
    whole_rows = whole[:block_rows]
    whole_gain = whole[block_rows].astype(jnp.float32)
    xfull = whole_rows.astype(jnp.float32)
    normed = (
        xfull
        * lax.rsqrt(jnp.mean(xfull * xfull, axis=1, keepdims=True) + 1e-06)
        * attn_norm_gain.astype(jnp.float32)
    ).astype(jnp.bfloat16)
    raw_pair = jnp.stack([project(w_query, normed), project(w_key, normed)]).astype(jnp.bfloat16)
    raw_pair = lax.optimization_barrier(raw_pair)
    for level in range(group.bit_length() - 1):
        partner = partner_2(raw_pair, "row", level)
        upper = row_index >> level & 1 == 1
        raw_pair = jnp.where(
            upper,
            jnp.concatenate([partner, raw_pair], axis=1),
            jnp.concatenate([raw_pair, partner], axis=1),
        )
    pair_f = raw_pair.astype(jnp.float32).reshape(2, local_heads, DK, block_rows)
    unit_pair = (
        pair_f * lax.rsqrt(jnp.sum(pair_f * pair_f, axis=2, keepdims=True) + 1e-06)
    ).astype(jnp.bfloat16)
    key_blocks = unit_pair.reshape(2, local_heads, col_count, key_rows, block_rows)
    swapped = swap_blocks(jnp.transpose(key_blocks, (2, 0, 1, 3, 4)), "col")
    tiles_qk = jnp.transpose(swapped, (1, 2, 3, 0, 4)).reshape(2, local_heads, key_rows, batch)
    query = tiles_qk[0].astype(jnp.float32)
    key = tiles_qk[1].astype(jnp.float32)
    unit_f = unit_pair.astype(jnp.float32)
    intersection = jnp.sum(unit_f[0] * unit_f[1], axis=1)
    value_t = project(w_value, normed)
    gate_t = project(w_gate, normed)
    decay_in = lax.dynamic_slice_in_dim(project(w_decay, normed), first_head, local_heads, 0)
    beta_in = lax.dynamic_slice_in_dim(project(w_beta, normed), first_head, local_heads, 0)
    rate = jnp.exp(lax.dynamic_slice_in_dim(decay_log, first_head, local_heads, 0))
    bias = lax.dynamic_slice_in_dim(decay_bias, first_head, local_heads, 0)
    alpha_t = jnp.exp(-rate[:, None] * jax.nn.softplus(decay_in + bias[:, None]))
    beta_t = jax.nn.sigmoid(beta_in)
    tiles = state.reshape(key_rows, local_heads, value_part, batch)
    value4 = value_t.reshape(local_heads, value_part, block_rows)
    key_major = jnp.transpose(key, (1, 0, 2))
    responses = jnp.stack(
        [
            jnp.einsum("khvb,hkb->hvb", tiles, key, precision=highest),
            jnp.einsum("khvb,hkb->hvb", tiles, query, precision=highest),
        ]
    )
    responses = responses.reshape(2, local_heads, value_part, col_count, block_rows)
    recall, answer = lax.psum_scatter(jnp.transpose(responses, (3, 0, 1, 2, 4)), "col", scatter_dimension=0, tiled=False)
    write = beta_t[:, None, :] * (value4 - alpha_t[:, None, :] * recall)
    parts = gather_blocks(
        jnp.concatenate([write.reshape(value_cols, block_rows), alpha_t], axis=0), "col"
    )
    parts = jnp.transpose(parts, (1, 0, 2)).reshape(value_cols + local_heads, batch)
    write_all = parts[:value_cols].reshape(local_heads, value_part, batch)
    alpha_all = parts[value_cols:]
    updated = alpha_all[None, :, None, :] * tiles + key_major[:, :, None, :] * write_all[None]
    readout = alpha_t[:, None, :] * answer + intersection[:, None, :] * write
    power = jnp.sum(readout * readout, axis=1)
    for level in range(group.bit_length() - 1):
        power = power + partner_2(power, "row", level)
    gain_part = lax.dynamic_slice_in_dim(head_gain, row_index % group * value_part, value_part, 0)
    gate4 = gate_t.reshape(local_heads, value_part, block_rows)
    mixed = (
        readout
        * lax.rsqrt(power / DV + 1e-05)[:, None, :]
        * gain_part[None, :, None]
        * jax.nn.silu(gate4)
    )
    mixed_heads = mixed.reshape(value_cols, block_rows).astype(jnp.bfloat16)
    share = -(-block_rows // row_count)
    extra = share * row_count - block_rows
    partial = lax.dot_general(
        mixed_heads, w_out, (((0,), (0,)), ((), ())), preferred_element_type=jnp.float32
    )
    branch = lax.psum_scatter(
        jnp.pad(partial, ((0, extra), (0, 0))).reshape(row_count, share, D),
        "row",
        scatter_dimension=0,
        tiled=False,
    )
    own_rows = lax.dynamic_slice_in_dim(
        jnp.pad(whole_rows, ((0, extra), (0, 0))), row_index * share, share, 0
    )
    hidden = own_rows.astype(jnp.float32) + branch
    energy = jnp.mean(hidden * hidden, axis=1, keepdims=True)
    final = (hidden * lax.rsqrt(energy + 1e-06) * whole_gain[None, :]).astype(jnp.bfloat16)
    tall = lax.all_gather(final, ("col", "row"), axis=0, tiled=True)
    if extra:
        tall = tall.reshape(col_count, share * row_count, D)[:, :block_rows].reshape(batch, D)
    logits = jnp.dot(tall, lm_weight, preferred_element_type=jnp.float32)
    vocab_start = (row_index * col_count + col_index) * vocab_dev
    hits = jnp.arange(vocab_dev, dtype=jnp.int32)[None, :] + vocab_start == token_ids[:, None]
    local_pick = jnp.sum(jnp.where(hits, logits, jnp.zeros_like(logits)), axis=1)
    local_top = jnp.max(logits, axis=1)
    expo = jnp.exp(logits - local_top[:, None])
    local_total = jnp.sum(expo, axis=1)
    local_weighted = jnp.sum(expo * logits, axis=1)
    stats = jnp.stack([local_top, local_total, local_weighted, local_pick])
    top, total, weighted, picked = merge_stats(merge_stats(stats, "col"), "row")
    lse = top + jnp.log(total)
    logprob = picked - lse
    entropy = lse - weighted / total
    gap = jnp.clip(ref_logprob - logprob, -20.0, 20.0)
    kl = jnp.minimum(jnp.exp(gap) - gap - 1.0, 10.0)
    new_state = updated.reshape(key_rows, value_cols, batch)
    return (new_state, logprob, entropy, kl)


def solution(mesh):
    in_specs = (
        P("col", "row"),
        P("col", "row", None),
        P(),
        P(None, "row"),
        P(None, "row"),
        P(None, "row"),
        P(None, "row"),
        P(),
        P(),
        P(),
        P(),
        P(),
        P("row", None),
        P("row"),
        P(None, ("row", "col")),
        P(),
        P(),
    )
    out_specs = (P("col", "row", None), P(), P(), P())
    return jax.shard_map(
        per_device, mesh=mesh, in_specs=in_specs, out_specs=out_specs, check_vma=False
    )
```

profile of v0, /device:TPU:0, one launch (start us, length us, event | category | flops | bytes accessed | tf_op | source)
XLA Modules:
  0.0 320.8 jit_solution(1117575225942106937)
XLA Ops:
  7.2 0.8 broadcast_in_dim.9
  8.0 1.6 pad_maximum_fusion.1
  9.8 0.7 convert_element_type.36
  10.5 26.9 %all-gather.8.cloned.1.call-done = bf16[289,2048]{1,0:T(8,128)(2,1)} async-done(((bf16[289,256]{1,0:T(8,128)(2,1)}), bf16[289,2048]{1,0:T(8,128)(2,1)}) %all-gather.8.cloned.1.call-update) | async-done | bytes 1183760 | tf_op jit(solution)/shard_map/all_gather | solution.py:112
  37.4 1.7 fusion.2
  39.1 1.6 fusion.4
  40.7 0.5 fusion.6
  41.2 0.6 copy-done.1
  41.8 0.6 copy-done.17
  42.4 0.5 fusion.5
  42.9 0.7 copy-done.5
  43.6 1.1 reshape.113
  44.7 1.1 copy.103
  45.9 2.5 multiply_reduce_fusion.3
  48.3 1.1 copy.104
  49.6 1.5 collective-permute-start
  51.2 2.4 collective-permute-start.2
  53.6 0.6 collective-permute-start.1
  54.2 2.9 collective-permute-done
  57.1 5.6 %collective-permute-done.1 = bf16[1,2,2,32,288]{4,3,0,2,1:T(8,128)(2,1)S(1)} collective-permute-done((bf16[1,2,2,32,288]{4,3,0,2,1:T(8,128)(2,1)S(1)}, bf16[1,2,2,32,288]{4,3,0,2,1:T(8,128)(2,1)S(1)}, u32[]{:S(2)}, u32[]{:S(2)}) %collective-permute-start.1) | collective-permute-done | bytes 73760 | tf_op jit(solution)/shard_map/ppermute | solution.py:38
  63.7 0.7 convert_bitcast_fusion
  64.6 17.3 %multiply_reduce_fusion.1 = (f32[2,1152,128]{1,2,0:T(8,128)}, f32[2,1152,128]{1,2,0:T(8,128)}) fusion(f32[2,1152,32,128]{1,3,0,2:T(8,128)} %bitcast.222, f32[2,1152,32]{1,0,2:T(2,128)S(1)} %copy.148, f32[2,1152,32]{1,0,2:T(2,128)S(1)} %copy.149), kind=kLoop, calls=%fused_computation.3 | loop fusion | flops 37158912 | bytes 40697856
  81.9 2.6 copy.130
  84.6 2.7 copy.138
  87.2 1.8 maximum_bitcast_fusion
  89.0 1.6 copy.107
  90.7 0.5 copy-done.18
  91.4 0.9 copy.114
  92.3 1.7 fusion.53
  94.3 2.0 fusion.52
  96.3 0.8 copy.146
  97.1 1.7 fusion.9
  99.3 37.5 %reduce-scatter.3.cloned.1.call-done = f32[1,2,2,128,288]{3,4,2,1,0:T(8,128)} async-done(((f32[4,2,2,128,288]{3,4,2,1,0:T(8,128)}), f32[1,2,2,128,288]{3,4,2,1,0:T(8,128)}) %reduce-scatter.3.cloned.1.call-update) | async-done | bytes 589840 | tf_op jit(solution)/shard_map/reduce_scatter | solution.py:160
  136.8 1.2 fusion.47
  138.0 0.9 copy.113
  140.0 0.5 fusion.15
  140.7 0.5 copy-done.6
  142.5 2.2 fusion.22
  144.8 3.2 %fusion.7 = f32[8,36,2048]{2,1,0:T(8,128)} fusion(bf16[8,36,256]{2,1,0:T(8,128)(2,1)S(1)} %dot_general.55, bf16[256,2048]{1,0:T(8,128)(2,1)} %param.29), kind=kOutput, calls=%fused_computation.19 | convolution fusion | flops 301989888 | bytes 3555328 | tf_op jit(solution)/shard_map/dot_general | solution.py:184
  148.1 2.5 slice.72
  150.6 0.8 slice_convert_fusion
  151.4 39.7 %reduce-scatter.5.cloned.1.call-done = f32[1,36,2048]{2,1,0:T(8,128)} async-done(((f32[8,36,2048]{2,1,0:T(8,128)}), f32[1,36,2048]{2,1,0:T(8,128)}) %reduce-scatter.5.cloned.1.call-update) | async-done | bytes 294928 | tf_op jit(solution)/shard_map/reduce_scatter | solution.py:187
  191.0 1.2 multiply_reduce_fusion.4
  192.3 1.8 fusion.23
  194.1 0.8 maximum_bitcast_fusion.1
  194.9 1.5 collective-permute-start.3
  196.3 2.4 collective-permute-start.4
  198.8 0.9 copy.111
  199.7 1.4 collective-permute-start.5
  201.3 10.6 %collective-permute-done.3 = f32[1,258,288]{1,2,0:T(8,128)} collective-permute-done((f32[1,258,288]{1,2,0:T(8,128)}, f32[1,258,288]{1,2,0:T(8,128)}, u32[]{:S(2)}, u32[]{:S(2)}) %collective-permute-start.3) | collective-permute-done | bytes 297248 | tf_op jit(solution)/shard_map/ppermute | solution.py:49
  211.9 1.0 constant_dynamic-update-slice_fusion.2
  212.9 18.4 %collective-permute-done.4 = f32[1,258,288]{1,2,0:T(8,128)} collective-permute-done((f32[1,258,288]{1,2,0:T(8,128)}, f32[1,258,288]{1,2,0:T(8,128)}, u32[]{:S(2)}, u32[]{:S(2)}) %collective-permute-start.4) | collective-permute-done | bytes 297248 | tf_op jit(solution)/shard_map/ppermute | solution.py:49
  231.3 1.0 constant_dynamic-update-slice_fusion.1
  232.5 1.1 slice.76
  233.6 2.7 copy.112
  236.6 1.2 copy-done.4
  237.8 28.8 %fusion = f32[32,256,1152]{2,1,0:T(8,128)} fusion(f32[32,256,1152]{2,1,0:T(8,128)} %param.18, f32[256,1152]{1,0:T(8,128)S(1)} %copy-done.4, f32[32,2,1152]{2,1,0:T(2,128)S(1)} %copy-done.8, f32[256,1152]{1,0:T(8,128)S(1)} %bitcast.230), kind=kLoop, calls=%fused_computation.1 | loop fusion | flops 28311552 | bytes 78151680 | tf_op jit(solution)/shard_map/add | solution.py:168
  266.6 9.4 %all-gather.10.cloned.1.call-done = bf16[32,36,2048]{2,1,0:T(8,128)(2,1)} async-done(((bf16[1,36,2048]{2,1,0:T(8,128)(2,1)}), bf16[32,36,2048]{2,1,0:T(8,128)(2,1)}) %all-gather.10.cloned.1.call-update) | async-done | bytes 4718608 | tf_op jit(solution)/shard_map/all_gather | solution.py:199
  276.0 7.2 %reshape.120 = bf16[1152,2048]{1,0:T(8,128)(2,1)} reshape(bf16[32,36,2048]{2,1,0:T(8,128)(2,1)} %all-gather.10.cloned.1.call-done) | data formatting | bytes 9437184
  283.2 6.2 %fusion.51 = (f32[1152]{0:T(1024)S(1)}, f32[1152,640]{0,1:T(8,128)S(1)}) fusion(bf16[1152,2048]{1,0:T(8,128)(2,1)} %reshape.120, bf16[2048,640]{1,0:T(8,128)(2,1)S(1)} %copy-done), kind=kOutput, calls=%fused_computation.118 | convolution fusion | flops 3020635136 | bytes 10293760 | tf_op jit(solution)/shard_map/dot_general | solution.py:202
  289.5 0.9 fusion.1
  290.5 13.5 %all-gather.3 = f32[4,4,1152]{2,1,0:T(4,128)S(1)} all-gather(f32[1,4,1152]{2,1,0:T(4,128)S(1)} %maximum_bitcast_fusion.2), channel_id=2, replica_groups=mesh['row'=8,'col'=4] {'col'}, dimensions={0}, use_global_device_ids=true | all-gather | bytes 92160 | tf_op jit(solution)/shard_map/all_gather | solution.py:65
  304.1 9.4 %all-gather.4 = f32[8,4,1152]{2,1,0:T(4,128)S(1)} all-gather(f32[1,4,1152]{2,1,0:T(4,128)S(1)} %maximum_bitcast_fusion.3), channel_id=3, replica_groups=mesh['row'=8,'col'=4] {'row'}, dimensions={0}, use_global_device_ids=true | all-gather | bytes 165888 | tf_op jit(solution)/shard_map/all_gather | solution.py:65
  313.7 0.6 fusion.35
  (102 shorter events, 6.0 us)
Async XLA Ops:
  7.2 276.1 %copy-start = (bf16[2048,640]{1,0:T(8,128)(2,1)S(1)}, bf16[2048,640]{1,0:T(8,128)(2,1)}, u32[]{:S(2)}) copy-start(bf16[2048,640]{1,0:T(8,128)(2,1)} %param.31) | copy-start | bytes 7864324
  7.2 30.2 %all-gather.8.cloned.1.call-start = ((), (), s32[]{:S(2)}) async-start(), calls=%async_computation.2 | async-start | bytes 1363968 | tf_op jit(solution)/shard_map/all_gather | solution.py:112
  9.6 127.2 %reduce-scatter.3.cloned.1.call-start = ((), (), s32[]{:S(2)}) async-start(), calls=%async_computation.3 | async-start | bytes 2949120 | tf_op jit(solution)/shard_map/reduce_scatter | solution.py:160
  37.4 3.3 %copy-start.16 = (bf16[2048,256]{1,0:T(8,128)(2,1)S(1)}, bf16[2048,256]{1,0:T(8,128)(2,1)}, u32[]{:S(2)}) copy-start(bf16[2048,256]{1,0:T(8,128)(2,1)} %param.21) | copy-start | bytes 3145732
  40.7 1.1 copy-start.1
  40.7 1.7 copy-start.17
  42.9 0.7 copy-start.5
  49.6 7.5 %collective-permute-start = (bf16[1,2,2,32,288]{4,3,0,2,1:T(8,128)(2,1)S(1)}, bf16[1,2,2,32,288]{4,3,0,2,1:T(8,128)(2,1)S(1)}, u32[]{:S(2)}, u32[]{:S(2)}) collective-permute-start(bf16[1,2,2,32,288]{4,3,0,2,1:T(8,128)(2,1)S(1)} %get-tuple-element.25), channel_id=1, source_target_pairs={{0,1},{1,2},{2,3},{3,0},{4,5},{5,6},{6,7},{7,4},{8,9},{9,10},{10,1... | collective-permute-start | bytes 221192 | tf_op jit(solution)/shard_map/ppermute | solution.py:38
  51.2 11.5 %collective-permute-start.2 = (bf16[1,2,2,32,288]{4,3,0,2,1:T(8,128)(2,1)S(1)}, bf16[1,2,2,32,288]{4,3,0,2,1:T(8,128)(2,1)S(1)}, u32[]{:S(2)}, u32[]{:S(2)}) collective-permute-start(bf16[1,2,2,32,288]{4,3,0,2,1:T(8,128)(2,1)S(1)} %get-tuple-element.23), channel_id=1, source_target_pairs={{0,3},{1,0},{2,1},{3,2},{4,7},{5,4},{6,5},{7,6},{8,11},{9,8},{10,9... | collective-permute-start | bytes 221192 | tf_op jit(solution)/shard_map/ppermute | solution.py:38
  53.6 9.1 %collective-permute-start.1 = (bf16[1,2,2,32,288]{4,3,0,2,1:T(8,128)(2,1)S(1)}, bf16[1,2,2,32,288]{4,3,0,2,1:T(8,128)(2,1)S(1)}, u32[]{:S(2)}, u32[]{:S(2)}) collective-permute-start(bf16[1,2,2,32,288]{4,3,0,2,1:T(8,128)(2,1)S(1)} %get-tuple-element.24), channel_id=1, source_target_pairs={{0,2},{1,3},{2,0},{3,1},{4,6},{5,7},{6,4},{7,5},{8,10},{9,11},{10,... | collective-permute-start | bytes 221192 | tf_op jit(solution)/shard_map/ppermute | solution.py:38
  90.6 0.7 copy-start.18
  90.6 0.7 copy-start.19
  90.6 0.8 copy-start.20
  90.6 1.7 copy-start.12
  90.6 3.7 %copy-start.13 = (bf16[2048,16]{0,1:T(8,128)(2,1)S(1)}, bf16[2048,16]{0,1:T(8,128)(2,1)}, u32[]{:S(2)}) copy-start(bf16[2048,16]{0,1:T(8,128)(2,1)} %param.25) | copy-start | bytes 196612
  90.6 6.5 %copy-start.3 = (f32[2,2,128,288]{2,1,3,0:T(2,128)S(1)}, f32[2,2,128,288]{2,1,3,0:T(2,128)}, u32[]{:S(2)}) copy-start(f32[2,2,128,288]{2,1,3,0:T(2,128)} %reshape.113) | copy-start | bytes 1769476
  90.7 100.4 %reduce-scatter.5.cloned.1.call-start = ((), (), s32[]{:S(2)}) async-start(), calls=%async_computation.4 | async-start | bytes 2949120 | tf_op jit(solution)/shard_map/reduce_scatter | solution.py:187
  98.8 40.4 %copy-start.11 = (f32[2,288]{0,1:T(8,128)S(1)}, f32[2,288]{0,1:T(8,128)}, u32[]{:S(2)}) copy-start(f32[2,288]{0,1:T(8,128)} %copy.146) | copy-start | bytes 6916
  136.8 3.2 copy-start.2
  136.8 3.2 copy-start.10
  140.0 0.7 copy-start.7
  140.0 1.2 copy-start.6
  148.0 128.0 %all-gather.10.cloned.1.call-start = ((), (), s32[]{:S(2)}) async-start(), calls=%async_computation.5 | async-start | bytes 5406720 | tf_op jit(solution)/shard_map/all_gather | solution.py:199
  148.1 50.7 %copy-start.9 = (f32[32,2,1152]{2,0,1:T(8,128)S(1)}, f32[32,2,1152]{2,0,1:T(8,128)}, u32[]{:S(2)}) copy-start(f32[32,2,1152]{2,0,1:T(8,128)} %get-tuple-element.31) | copy-start | bytes 884740
  194.9 17.0 %collective-permute-start.3 = (f32[1,258,288]{1,2,0:T(8,128)}, f32[1,258,288]{1,2,0:T(8,128)}, u32[]{:S(2)}, u32[]{:S(2)}) collective-permute-start(f32[1,258,288]{1,2,0:T(8,128)} %maximum_bitcast_fusion.1), channel_id=1, source_target_pairs={{0,1},{1,2},{2,3},{3,0},{4,5},{5,6},{6,7},{7,4},{8,9},{9,10},{10,1... | collective-permute-start | bytes 891656 | tf_op jit(solution)/shard_map/ppermute | solution.py:49
  196.3 35.0 %collective-permute-start.4 = (f32[1,258,288]{1,2,0:T(8,128)}, f32[1,258,288]{1,2,0:T(8,128)}, u32[]{:S(2)}, u32[]{:S(2)}) collective-permute-start(f32[1,258,288]{1,2,0:T(8,128)} %maximum_bitcast_fusion.1), channel_id=1, source_target_pairs={{0,2},{1,3},{2,0},{3,1},{4,6},{5,7},{6,4},{7,5},{8,10},{9,11},{10,... | collective-permute-start | bytes 891656 | tf_op jit(solution)/shard_map/ppermute | solution.py:49
  199.7 32.6 %collective-permute-start.5 = (f32[1,258,288]{1,2,0:T(8,128)}, f32[1,258,288]{1,2,0:T(8,128)S(1)}, u32[]{:S(2)}, u32[]{:S(2)}) collective-permute-start(f32[1,258,288]{1,2,0:T(8,128)} %maximum_bitcast_fusion.1), channel_id=1, source_target_pairs={{0,3},{1,0},{2,1},{3,2},{4,7},{5,4},{6,5},{7,6},{8,11},{9,8},{10,9... | collective-permute-start | bytes 891656 | tf_op jit(solution)/shard_map/ppermute | solution.py:49
  233.6 3.0 copy-start.8
  236.5 1.3 copy-start.4
  283.2 6.2 %copy-start.14 = (s32[1152]{0:T(1024)S(1)}, s32[1152]{0:T(1024)}, u32[]{:S(2)}) copy-start(s32[1152]{0:T(1024)} %param.32) | copy-start | bytes 13828
  289.5 24.2 %copy-start.15 = (f32[1152]{0:T(1024)S(1)}, f32[1152]{0:T(1024)}, u32[]{:S(2)}) copy-start(f32[1152]{0:T(1024)} %param.33) | copy-start | bytes 13828
Sparse Core Ops, SparseCore 0:
  10.4 26.9 all-gather.7
  90.8 45.9 reduce-scatter.2
  148.2 42.8 reduce-scatter.4
  194.2 81.7 all-gather.9
where the time goes:
time: 322 us; the launch traced here: 321 us
  waiting for transfers between devices  151 us (47%)
  other arithmetic  66.1 us (21%)
  local copies, waits for them, and re-layouts  39.7 us (12%)
  blocking collectives  22.8 us (7%)
  matrix products  16.8 us (5%)
  between operations  14.4 us (4%)
  starting transfers between devices  10 us (3%)
    reduce_scatter x1, waiting for transfers between devices, per_device(): lax.psum_scatter(jnp.pad(partial, ((0, extra), (0, 0))).reshape(row_count...  39.7 us
    reduce_scatter x1, waiting for transfers between devices, per_device(): lax.psum_scatter(jnp.transpose(responses, (3, 0, 1, 2, 4)), 'col', scatte...  37.5 us
    ppermute x3, waiting for transfers between devices, gather_blocks(): got = lax.ppermute(block[None], axis, shift_pairs(count, step))  29 us
    add x1, other arithmetic, per_device(): alpha_all[None, :, None, :] * tiles  28.8 us
    all_gather x1, waiting for transfers between devices, per_device(): whole = lax.all_gather(packed, 'row', axis=1, tiled=True)  26.9 us
    all_gather x2, blocking collectives, merge_stats(): every = lax.all_gather(stats, axis, axis=0, tiled=False)  22.8 us
    unnamed x5, other arithmetic  19.2 us
    unnamed x47, local copies, waits for them, and re-layouts  13 us
  transfers between devices with their start and end apart: 10, of which 8 were waited for; matrix products, arithmetic and copies ran while one was open for 15% of the time, Pallas kernels for 0%

commit v1 on v0

--- a/solution.py
+++ b/solution.py
@@ -1,12 +1,17 @@
+import functools
+
 import jax
 import jax.numpy as jnp
 from jax import lax
+from jax.experimental import pallas as pl
+from jax.experimental.pallas import tpu as pltpu
 from jax.sharding import PartitionSpec as P
 
 D = 2048
 HEADS = 16
 DK = 128
 DV = 128
+LANES = 128
 
 
 def partner_2(block, axis, apart):
@@ -218,6 +223,557 @@
     return (new_state, logprob, entropy, kl)
 
 
+MESH_IDS = pl.DeviceIdType.MESH
+
+
+def remote(src, dst, send_sem, recv_sem, device):
+    return pltpu.make_async_remote_copy(
+        src_ref=src, dst_ref=dst, send_sem=send_sem, recv_sem=recv_sem,
+        device_id=device, device_id_type=MESH_IDS,
+    )
+
+
+def meet(peers):
+    barrier = pltpu.get_barrier_semaphore()
+    for peer in peers:
+        pl.semaphore_signal(barrier, inc=1, device_id=peer, device_id_type=MESH_IDS)
+    pl.semaphore_wait(barrier, len(peers))
+
+
+def places(rows, cols):
+    me_r, me_c = lax.axis_index("row"), lax.axis_index("col")
+    mate = me_r + 1 - 2 * lax.rem(me_r, 2)
+    return me_r, me_c, mate
+
+
+def all_peers(rows, cols):
+    me_r, me_c, _ = places(rows, cols)
+    peers = [(lax.rem(me_r + step, rows), me_c) for step in range(1, rows)]
+    return peers + [(me_r, lax.rem(me_c + step, cols)) for step in range(1, cols)]
+
+
+def row_gather_start(slots, rows, cols, send, recv):
+    me_r, me_c, mate = places(rows, cols)
+    chips = rows // 2
+    copies = []
+    for j in range(1, chips):
+        peer = lax.rem(me_r + 2 * j, rows)
+        copies.append(remote(slots.at[me_r], slots.at[me_r], send.at[j], recv.at[j], (peer, me_c)))
+    own = remote(slots.at[me_r], slots.at[me_r], send.at[0], recv.at[0], (mate, me_c))
+    for copy in copies:
+        copy.start()
+    own.start()
+    return own, copies
+
+
+def row_gather_finish(slots, rows, cols, send, recv, own, copies):
+    me_r, me_c, mate = places(rows, cols)
+    chips = rows // 2
+    passed = []
+    for j in range(1, chips):
+        copies[j - 1].wait_recv()
+        source = lax.rem(me_r + rows - 2 * j, rows)
+        copy = remote(
+            slots.at[source], slots.at[source], send.at[chips + j], recv.at[chips + j], (mate, me_c)
+        )
+        copy.start()
+        passed.append(copy)
+    own.wait_recv()
+    for copy in passed:
+        copy.wait_recv()
+    for copy in [own] + copies + passed:
+        copy.wait_send()
+
+
+def first_kernel(
+    rows, cols, heads, key_rows,
+    hid, gain, w4_hbm, w5_hbm, w6_hbm, w7_hbm, w_decay, w_beta, decay_log, decay_bias,
+    qk_out, value_out, gate_out, scal_out, alpha_out,
+    xg, normed, weights, blocks, w_sem, row_send, row_recv, col_send, col_recv, a_send, a_recv,
+):
+    me_r, me_c, mate = places(rows, cols)
+    count, width = hid.shape
+    loads = []
+    for index, source in enumerate((w4_hbm, w5_hbm, w6_hbm, w7_hbm)):
+        load = pltpu.make_async_copy(source, weights.at[index], w_sem.at[index])
+        load.start()
+        loads.append(load)
+    xg[me_r] = hid[...]
+    meet(all_peers(rows, cols))
+    own, copies = row_gather_start(xg, rows, cols, row_send, row_recv)
+    row_gather_finish(xg, rows, cols, row_send, row_recv, own, copies)
+    power = jnp.zeros((count, 1), jnp.float32)
+    for r in range(rows):
+        block = xg[r].astype(jnp.float32)
+        power = power + jnp.sum(block * block, axis=1, keepdims=True)
+    scale = lax.rsqrt(power / (rows * width) + 1e-06)
+    for r in range(rows):
+        block = xg[r].astype(jnp.float32)
+        normed[:, r * width:(r + 1) * width] = (
+            block * scale * gain[r * width:(r + 1) * width][None, :].astype(jnp.float32)
+        ).astype(jnp.bfloat16)
+    units, products = [], []
+    for index in range(2):
+        loads[index].wait()
+        raw = jnp.dot(normed[...], weights[index], preferred_element_type=jnp.float32)
+        raw = raw.astype(jnp.bfloat16).astype(jnp.float32)
+        for h in range(heads):
+            part = raw[:, h * DK:(h + 1) * DK]
+            unit = part * lax.rsqrt(jnp.sum(part * part, axis=1, keepdims=True) + 1e-06)
+            units.append(unit.astype(jnp.bfloat16))
+    line = 2 * heads * key_rows
+    total = 2 * heads * DK
+    given = lax.broadcasted_iota(jnp.int32, (total, total), 0)
+    taken = lax.broadcasted_iota(jnp.int32, (total, total), 1)
+    inside = lax.rem(taken, line)
+    wanted = inside // key_rows * DK + taken // line * key_rows + lax.rem(inside, key_rows)
+    select = jnp.where(given == wanted, 1.0, 0.0).astype(jnp.bfloat16)
+    packed = jnp.dot(
+        jnp.concatenate(units, axis=1), select, preferred_element_type=jnp.float32
+    ).astype(jnp.bfloat16)
+    for c in range(cols):
+        blocks[c] = packed[:, c * line:(c + 1) * line]
+    qk_copies = []
+    for step in range(1, cols):
+        peer = lax.rem(me_c + step, cols)
+        copy = remote(blocks.at[peer], qk_out.at[me_c], col_send.at[step], col_recv.at[step], (me_r, peer))
+        copy.start()
+        qk_copies.append(copy)
+    qk_out[me_c] = blocks[me_c]
+    over = (((1,), (1,)), ((), ()))
+    decay_in = lax.dot_general(normed[...], w_decay[...], over, preferred_element_type=jnp.float32)
+    beta_in = lax.dot_general(normed[...], w_beta[...], over, preferred_element_type=jnp.float32)
+    z = decay_in + decay_bias[...]
+    soft = jnp.maximum(z, 0.0) + jnp.log1p(jnp.exp(-jnp.abs(z)))
+    alpha16 = jnp.exp(-jnp.exp(decay_log[...]) * soft)
+    beta16 = 1.0 / (1.0 + jnp.exp(-beta_in))
+    column = lax.broadcasted_iota(jnp.int32, alpha16.shape, 1)
+    lane = lax.broadcasted_iota(jnp.int32, scal_out.shape, 1)
+    scal = jnp.zeros(scal_out.shape, jnp.float32)
+    for h in range(heads):
+        mine = column == me_r * heads + h
+        alpha = jnp.sum(jnp.where(mine, alpha16, 0.0), axis=1, keepdims=True)
+        beta = jnp.sum(jnp.where(mine, beta16, 0.0), axis=1, keepdims=True)
+        inter = jnp.sum(
+            units[h].astype(jnp.float32) * units[heads + h].astype(jnp.float32), axis=1, keepdims=True
+        )
+        scal = jnp.where(lane == h, alpha, scal)
+        scal = jnp.where(lane == heads + h, beta, scal)
+        scal = jnp.where(lane == 2 * heads + h, inter, scal)
+    scal_out[...] = scal
+    alpha_out[me_c] = jnp.transpose(scal)[0:8, :]
+    a_copies = []
+    for step in range(1, cols):
+        peer = lax.rem(me_c + step, cols)
+        copy = remote(alpha_out.at[me_c], alpha_out.at[me_c], a_send.at[step], a_recv.at[step], (me_r, peer))
+        copy.start()
+        a_copies.append(copy)
+    loads[2].wait()
+    value_out[...] = jnp.dot(normed[...], weights[2], preferred_element_type=jnp.float32)
+    loads[3].wait()
+    gate_out[...] = jnp.dot(normed[...], weights[3], preferred_element_type=jnp.float32)
+    for copy in qk_copies + a_copies:
+        copy.wait()
+
+
+def response_kernel(heads, key_rows, tile, cols, state, qk, recall_out, answer_out, key_out, qk_t, acc):
+    step = pl.program_id(0)
+    per_head = DV // tile
+    batch = state.shape[2]
+    count = batch // cols
+    h = step // per_head
+
+    @pl.when(step == 0)
+    def _():
+        for c in range(batch // LANES):
+            part = qk[c * LANES:(c + 1) * LANES, :].astype(jnp.float32)
+            qk_t[:, c * LANES:(c + 1) * LANES] = jnp.transpose(part)
+        key_out[...] = qk_t[heads * key_rows:, :]
+
+    v0 = pl.multiple_of(lax.rem(step, per_head) * tile, tile)
+    q0 = pl.multiple_of(h * key_rows, key_rows)
+    k0 = pl.multiple_of((heads + h) * key_rows, key_rows)
+
+    def lanes_step(c, _):
+        lanes = pl.ds(pl.multiple_of(c * LANES, LANES), LANES)
+        keys = qk_t[pl.ds(k0, key_rows), lanes]
+        queries = qk_t[pl.ds(q0, key_rows), lanes]
+        recall = jnp.zeros((tile, LANES), jnp.float32)
+        answer = jnp.zeros((tile, LANES), jnp.float32)
+        for k in range(key_rows):
+            cell = state[k, :, lanes]
+            recall = recall + cell * keys[k:k + 1]
+            answer = answer + cell * queries[k:k + 1]
+        acc[0, pl.ds(v0, tile), lanes] = recall
+        acc[1, pl.ds(v0, tile), lanes] = answer
+        return 0
+
+    lax.fori_loop(0, batch // LANES, lanes_step, 0)
+
+    @pl.when(lax.rem(step, per_head) == per_head - 1)
+    def _():
+        head = pl.ds(pl.multiple_of(h * DV, DV), DV)
+        for t, out in enumerate((recall_out, answer_out)):
+            flat = jnp.transpose(acc[t]).astype(out.dtype)
+            for c in range(cols):
+                out[c, :, head] = flat[c * count:(c + 1) * count, :]
+
+
+def update_kernel(heads, key_rows, tile, state, key, alpha, write, out, write_t, alpha_t):
+    step = pl.program_id(0)
+    per_head = DV // tile
+    batch = state.shape[2]
+    h = step // per_head
+
+    @pl.when(step == 0)
+    def _():
+        for c in range(batch // LANES):
+            part = write[c * LANES:(c + 1) * LANES, :].astype(jnp.float32)
+            write_t[:, c * LANES:(c + 1) * LANES] = jnp.transpose(part)
+        every = jnp.concatenate([alpha[c] for c in range(alpha.shape[0])], axis=1)
+        for n in range(heads):
+            alpha_t[8 * n:8 * n + 8, :] = jnp.broadcast_to(every[n:n + 1], (8, batch))
+
+    rows = pl.ds(pl.multiple_of(step * tile, tile), tile)
+    k0 = pl.multiple_of(h * key_rows, key_rows)
+    a0 = pl.multiple_of(h * 8, 8)
+
+    def lanes_step(c, _):
+        lanes = pl.ds(pl.multiple_of(c * LANES, LANES), LANES)
+        fade = alpha_t[pl.ds(a0, 8), lanes][0:1]
+        new = write_t[rows, lanes]
+        keys = key[pl.ds(k0, key_rows), lanes]
+        for k in range(key_rows):
+            out[k, :, lanes] = fade * state[k, :, lanes] + keys[k:k + 1] * new
+        return 0
+
+    lax.fori_loop(0, batch // LANES, lanes_step, 0)
+
+
+def last_kernel(
+    rows, cols, heads,
+    recalls, answers, value, gate, scal, head_gain, hid, w_out, final_gain, lm_hbm, tokens, ref_logprob,
+    write_g, logprob_out, entropy_out, kl_out,
+    lm, token_cols, recall_in, answer_in, w_cols, mixed_g, energy, tall, logits, stats, stats_z,
+    lm_sem, rs_send, rs_recv, an_send, an_recv, wo_send, wo_recv, wr_send, wr_recv, mx_send, mx_recv,
+    en_send, en_recv, z_send, z_recv, r_send, r_recv, m_send, m_recv, s_send, s_recv, t_send, t_recv,
+):
+    me_r, me_c, mate = places(rows, cols)
+    chips = rows // 2
+    count, width = hid.shape
+    load = pltpu.make_async_copy(lm_hbm, lm, lm_sem)
+    load.start()
+    meet(all_peers(rows, cols))
+    rs_copies = []
+    for step in range(1, cols):
+        peer = lax.rem(me_c + step, cols)
+        for source, target, send, recv in (
+            (recalls, recall_in, rs_send, rs_recv), (answers, answer_in, an_send, an_recv)
+        ):
+            copy = remote(source.at[peer], target.at[step - 1], send.at[step], recv.at[step], (me_r, peer))
+            copy.start()
+            rs_copies.append(copy)
+    wo_copies = []
+    for step in range(1, rows):
+        peer = lax.rem(me_r + step, rows)
+        columns = pl.ds(pl.multiple_of(peer * width, LANES), width)
+        copy = remote(w_out.at[:, columns], w_cols.at[me_r], wo_send.at[step], wo_recv.at[step], (peer, me_c))
+        copy.start()
+        wo_copies.append(copy)
+    w_cols[me_r] = w_out[:, pl.ds(pl.multiple_of(me_r * width, LANES), width)]
+    batch = tokens.shape[0]
+    for c in range(batch // LANES):
+        piece = tokens[c * LANES:(c + 1) * LANES][None, :]
+        token_cols[c * LANES:(c + 1) * LANES, :] = jnp.transpose(jnp.broadcast_to(piece, (LANES, LANES)))
+    for copy in rs_copies:
+        copy.wait_recv()
+    total = []
+    for source, target in ((recalls, recall_in), (answers, answer_in)):
+        part = source[me_c].astype(jnp.float32)
+        for step in range(cols - 1):
+            part = part + target[step].astype(jnp.float32)
+        total.append(part)
+    pieces = []
+    for h in range(heads):
+        span = slice(h * DV, (h + 1) * DV)
+        alpha = scal[:, h:h + 1]
+        beta = scal[:, heads + h:heads + h + 1]
+        inter = scal[:, 2 * heads + h:2 * heads + h + 1]
+        write = beta * (value[:, span] - alpha * total[0][:, span])
+        write_g[me_c, :, span] = write.astype(jnp.bfloat16)
+        readout = alpha * total[1][:, span] + inter * write
+        power = jnp.sum(readout * readout, axis=1, keepdims=True)
+        gates = gate[:, span]
+        silu = gates * (1.0 / (1.0 + jnp.exp(-gates)))
+        mixed = readout * lax.rsqrt(power / DV + 1e-05) * head_gain[...][None, :] * silu
+        mixed_g[me_r, :, span] = mixed.astype(jnp.bfloat16)
+    wr_copies = []
+    for step in range(1, cols):
+        peer = lax.rem(me_c + step, cols)
+        copy = remote(write_g.at[me_c], write_g.at[me_c], wr_send.at[step], wr_recv.at[step], (me_r, peer))
+        copy.start()
+        wr_copies.append(copy)
+    own, copies = row_gather_start(mixed_g, rows, cols, mx_send, mx_recv)
+    for copy in wo_copies:
+        copy.wait_recv()
+    row_gather_finish(mixed_g, rows, cols, mx_send, mx_recv, own, copies)
+    hidden = hid[...].astype(jnp.float32)
+    branch = jnp.zeros((count, width), jnp.float32)
+    for r in range(rows):
+        branch = branch + jnp.dot(mixed_g[r], w_cols[r], preferred_element_type=jnp.float32)
+    hidden = hidden + branch
+    own_energy = jnp.broadcast_to(jnp.sum(hidden * hidden, axis=1, keepdims=True), (count, LANES))
+    energy[me_r] = jnp.transpose(own_energy)[0:8, :]
+    en_copies = []
+    for step in range(1, rows):
+        peer = lax.rem(me_r + step, rows)
+        copy = remote(energy.at[me_r], energy.at[me_r], en_send.at[step], en_recv.at[step], (peer, me_c))
+        copy.start()
+        en_copies.append(copy)
+    for copy in en_copies:
+        copy.wait_recv()
+    summed = energy[0]
+    for r in range(1, rows):
+        summed = summed + energy[r]
+    spread = jnp.transpose(jnp.concatenate([summed] * (LANES // 8), axis=0))[:, 0:1]
+    final = hidden * lax.rsqrt(spread / (rows * width) + 1e-06) * final_gain[...][None, :].astype(jnp.float32)
+    tall[me_r, me_c] = final.astype(jnp.bfloat16)
+
+    z_copies, r_copies, m_copies = [], {}, {}
+
+    def hand_on(source_c, place):
+        block = tall.at[me_r, source_c]
+        for j in range(1, chips):
+            peer = lax.rem(me_r + 2 * j, rows)
+            copy = remote(block, block, r_send.at[j, place], r_recv.at[j, place], (peer, me_c))
+            copy.start()
+            r_copies[j, place] = copy
+
+    def to_mate(source_r, source_c, j, place):
+        block = tall.at[source_r, source_c]
+        copy = remote(block, block, m_send.at[j, place], m_recv.at[j, place], (mate, me_c))
+        copy.start()
+        m_copies[j, place] = copy
+
+    def column(place):
+        return lax.rem(me_c + cols - place, cols)
+
+    for step in range(1, cols):
+        peer = lax.rem(me_c + step, cols)
+        block = tall.at[me_r, me_c]
+        copy = remote(block, block, z_send.at[step], z_recv.at[step], (me_r, peer))
+        copy.start()
+        z_copies.append(copy)
+    hand_on(me_c, 0)
+    to_mate(me_r, me_c, 0, 0)
+    for copy in wr_copies:
+        copy.wait_recv()
+    for place in range(1, cols):
+        z_copies[place - 1].wait_recv()
+        hand_on(column(place), place)
+        to_mate(me_r, column(place), 0, place)
+    load.wait()
+
+    def multiply(r, first):
+        block = lm[pl.ds(pl.multiple_of(r * width, width), width), :]
+
+        def one(c, _):
+            product = jnp.dot(tall[r, c], block, preferred_element_type=jnp.float32)
+            logits[c] = product if first else logits[c] + product
+            return 0
+
+        lax.fori_loop(0, cols, one, 0)
+
+    multiply(me_r, True)
+    for place in range(cols):
+        m_copies[0, place].wait_recv()
+    multiply(mate, False)
+    for j in range(1, chips):
+        source = lax.rem(me_r + rows - 2 * j, rows)
+        for place in range(cols):
+            r_copies[j, place].wait_recv()
+            to_mate(source, column(place), j, place)
+        multiply(source, False)
+        for place in range(cols):
+            m_copies[j, place].wait_recv()
+        multiply(lax.rem(mate + rows - 2 * j, rows), False)
+
+    vocab = lm.shape[1]
+    vocab_start = (me_r * cols + me_c) * vocab
+    turned = []
+    for c in range(cols):
+        part = logits[c]
+        at = lax.broadcasted_iota(jnp.int32, part.shape, 1) + vocab_start
+        hits = at == token_cols[c * count:(c + 1) * count, 0:1]
+        pick = jnp.sum(jnp.where(hits, part, 0.0), axis=1, keepdims=True)
+        top = jnp.max(part, axis=1, keepdims=True)
+        expo = jnp.exp(part - top)
+        mass = jnp.sum(expo, axis=1, keepdims=True)
+        weighted = jnp.sum(expo * part, axis=1, keepdims=True)
+        lane = lax.broadcasted_iota(jnp.int32, (count, LANES), 1)
+        cell = jnp.where(lane == 0, top, jnp.where(lane == 1, mass, jnp.where(lane == 2, weighted, pick)))
+        turned.append(jnp.transpose(cell)[0:4, :])
+    stats[me_r] = jnp.concatenate(turned, axis=1)
+
+    def merge(slots, number):
+        top = slots[0, 0:1, :]
+        for n in range(1, number):
+            top = jnp.maximum(top, slots[n, 0:1, :])
+        mass = jnp.zeros_like(top)
+        weighted = jnp.zeros_like(top)
+        pick = jnp.zeros_like(top)
+        for n in range(number):
+            shrink = jnp.exp(slots[n, 0:1, :] - top)
+            mass = mass + slots[n, 1:2, :] * shrink
+            weighted = weighted + slots[n, 2:3, :] * shrink
+            pick = pick + slots[n, 3:4, :]
+        return top, mass, weighted, pick
+
+    s_copies = []
+    for step in range(1, rows):
+        peer = lax.rem(me_r + step, rows)
+        copy = remote(stats.at[me_r], stats.at[me_r], s_send.at[step], s_recv.at[step], (peer, me_c))
+        copy.start()
+        s_copies.append(copy)
+    for copy in s_copies:
+        copy.wait_recv()
+    stats_z[me_c] = jnp.concatenate(merge(stats, rows), axis=0)
+    t_copies = []
+    for step in range(1, cols):
+        peer = lax.rem(me_c + step, cols)
+        copy = remote(stats_z.at[me_c], stats_z.at[me_c], t_send.at[step], t_recv.at[step], (me_r, peer))
+        copy.start()
+        t_copies.append(copy)
+    for copy in t_copies:
+        copy.wait_recv()
+    top, mass, weighted, pick = merge(stats_z, cols)
+    lse = top + jnp.log(mass)
+    logprob = pick - lse
+    logprob_out[...] = logprob.reshape(batch)
+    entropy_out[...] = (lse - weighted / mass).reshape(batch)
+    gap = jnp.clip(ref_logprob[...][None, :] - logprob, -20.0, 20.0)
+    kl_out[...] = jnp.minimum(jnp.exp(gap) - gap - 1.0, 10.0).reshape(batch)
+    for copy in rs_copies + wo_copies + wr_copies + en_copies + z_copies + s_copies + t_copies:
+        copy.wait_send()
+    for copy in list(r_copies.values()) + list(m_copies.values()):
+        copy.wait_send()
+
+
+def fused_device(
+    hidden_in, state, attn_norm_gain, w_query, w_key, w_value, w_gate, w_decay, w_beta, decay_log,
+    decay_bias, head_gain, w_out, final_gain, lm_weight, token_ids, ref_logprob,
+):
+    rows = lax.axis_size("row")
+    cols = lax.axis_size("col")
+    heads = HEADS // rows
+    count, width = hidden_in.shape
+    key_rows, value_cols, batch = state.shape
+    vocab = lm_weight.shape[1]
+    line = 2 * heads * key_rows
+    bf16, f32 = jnp.bfloat16, jnp.float32
+    vmem = pl.BlockSpec(memory_space=pltpu.VMEM)
+    hbm = pl.BlockSpec(memory_space=pl.ANY)
+    dma = pltpu.SemaphoreType.DMA
+    qk, value, gate, scal, alpha = pl.pallas_call(
+        functools.partial(first_kernel, rows, cols, heads, key_rows),
+        out_shape=[
+            jax.ShapeDtypeStruct((cols, count, line), bf16),
+            jax.ShapeDtypeStruct((count, value_cols), f32),
+            jax.ShapeDtypeStruct((count, value_cols), f32),
+            jax.ShapeDtypeStruct((count, LANES), f32),
+            jax.ShapeDtypeStruct((cols, 8, count), f32),
+        ],
+        in_specs=[vmem, vmem] + [hbm] * 4 + [vmem] * 4,
+        out_specs=[vmem] * 5,
+        scratch_shapes=[
+            pltpu.VMEM((rows, count, width), bf16),
+            pltpu.VMEM((count, rows * width), bf16),
+            pltpu.VMEM((4,) + w_query.shape, bf16),
+            pltpu.VMEM((cols, count, line), bf16),
+            dma((4,)), dma((rows,)), dma((rows,)), dma((cols,)), dma((cols,)), dma((cols,)), dma((cols,)),
+        ],
+        compiler_params=pltpu.CompilerParams(collective_id=0, has_side_effects=True),
+        name="first",
+    )(
+        hidden_in, attn_norm_gain, w_query, w_key, w_value, w_gate, w_decay.T, w_beta.T,
+        decay_log[None, :], decay_bias[None, :],
+    )
+    tile = 32
+    steps = value_cols // tile
+    block = pl.BlockSpec((key_rows, tile, batch), lambda i: (0, i, 0))
+    recalls, answers, key = pl.pallas_call(
+        functools.partial(response_kernel, heads, key_rows, tile, cols),
+        grid=(steps,),
+        out_shape=[
+            jax.ShapeDtypeStruct((cols, count, value_cols), bf16),
+            jax.ShapeDtypeStruct((cols, count, value_cols), f32),
+            jax.ShapeDtypeStruct((heads * key_rows, batch), f32),
+        ],
+        in_specs=[block, pl.BlockSpec((batch, line), lambda i: (0, 0))],
+        out_specs=[
+            pl.BlockSpec((cols, count, value_cols), lambda i: (0, 0, 0)),
+            pl.BlockSpec((cols, count, value_cols), lambda i: (0, 0, 0)),
+            pl.BlockSpec((heads * key_rows, batch), lambda i: (0, 0)),
+        ],
+        scratch_shapes=[pltpu.VMEM((line, batch), f32), pltpu.VMEM((2, DV, batch), f32)],
+        compiler_params=pltpu.CompilerParams(dimension_semantics=("arbitrary",)),
+        name="responses",
+    )(state, qk.reshape(batch, line))
+    write, logprob, entropy, kl = pl.pallas_call(
+        functools.partial(last_kernel, rows, cols, heads),
+        out_shape=[jax.ShapeDtypeStruct((cols, count, value_cols), bf16)]
+        + [jax.ShapeDtypeStruct((batch,), f32)] * 3,
+        in_specs=[vmem] * 9 + [hbm] + [vmem] * 2,
+        out_specs=[vmem] * 4,
+        scratch_shapes=[
+            pltpu.VMEM(lm_weight.shape, bf16),
+            pltpu.VMEM((batch, LANES), jnp.int32),
+            pltpu.VMEM((cols - 1, count, value_cols), bf16),
+            pltpu.VMEM((cols - 1, count, value_cols), f32),
+            pltpu.VMEM((rows, value_cols, width), bf16),
+            pltpu.VMEM((rows, count, value_cols), bf16),
+            pltpu.VMEM((rows, 8, count), f32),
+            pltpu.VMEM((rows, cols, count, width), bf16),
+            pltpu.VMEM((cols, count, vocab), f32),
+            pltpu.VMEM((rows, 4, batch), f32),
+            pltpu.VMEM((cols, 4, batch), f32),
+            dma(()), dma((cols,)), dma((cols,)),
+            dma((cols,)), dma((cols,)), dma((rows,)), dma((rows,)), dma((cols,)), dma((cols,)),
+            dma((rows,)), dma((rows,)), dma((rows,)), dma((rows,)), dma((cols,)), dma((cols,)),
+            dma((rows // 2, cols)), dma((rows // 2, cols)), dma((rows // 2, cols)), dma((rows // 2, cols)),
+            dma((rows,)), dma((rows,)), dma((cols,)), dma((cols,)),
+        ],
+        compiler_params=pltpu.CompilerParams(collective_id=1, has_side_effects=True),
+        name="last",
+    )(
+        recalls, answers, value, gate, scal, head_gain, hidden_in, w_out, final_gain, lm_weight,
+        token_ids, ref_logprob,
+    )
+    new_state = pl.pallas_call(
+        functools.partial(update_kernel, heads, key_rows, tile),
+        grid=(steps,),
+        out_shape=jax.ShapeDtypeStruct(state.shape, f32),
+        in_specs=[
+            block,
+            pl.BlockSpec(key.shape, lambda i: (0, 0)),
+            pl.BlockSpec(alpha.shape, lambda i: (0, 0, 0)),
+            pl.BlockSpec((batch, value_cols), lambda i: (0, 0)),
+        ],
+        out_specs=block,
+        scratch_shapes=[pltpu.VMEM((value_cols, batch), f32), pltpu.VMEM((8 * heads, batch), f32)],
+        compiler_params=pltpu.CompilerParams(dimension_semantics=("arbitrary",)),
+        name="update",
+    )(state, key, alpha, write.reshape(batch, value_cols))
+    return new_state, logprob, entropy, kl
+
+
+def fits(mesh):
+    rows, cols = mesh.shape["row"], mesh.shape["col"]
+    if rows % 2 or HEADS % rows or DK % cols:
+        return False
+    return 2 * (HEADS // rows) * (DK // cols) % LANES == 0
+
+
 def solution(mesh):
     in_specs = (
         P("col", "row"),
@@ -240,5 +796,5 @@
     )
     out_specs = (P("col", "row", None), P(), P(), P())
     return jax.shard_map(
-        per_device, mesh=mesh, in_specs=in_specs, out_specs=out_specs, check_vma=False
-    )
+        fused_device if fits(mesh) else per_device, mesh=mesh, in_specs=in_specs, out_specs=out_specs, check_vma=False
+    )

time: 322 us -> 184 us (0.57)
  Pallas kernels: 0 us -> 181 us
  waiting for transfers between devices: 151 us -> 0 us
  other arithmetic: 66.1 us -> 0 us
  local copies, waits for them, and re-layouts: 39.7 us -> 1.81 us
  blocking collectives: 22.8 us -> 0 us
  matrix products: 16.8 us -> 0 us
  between operations: 14.4 us -> 0.68 us
  starting transfers between devices: 10 us -> 0 us
    pallas_call x0 -> x4, Pallas kernels: none -> 181 us  [the longest x1 109 us: fused_device(): pl.pallas_call(functools.partial(last_kernel, rows, cols, heads), out_sha...]
    reduce_scatter x2 -> x0, waiting for transfers between devices: 77.2 us -> none  [the longest x1 39.7 us: per_device(): lax.psum_scatter(jnp.pad(partial, ((0, extra), (0, 0))).reshape(row_count...]
    ppermute x6 -> x0, waiting for transfers between devices: 37.4 us -> none  [the longest x3 29 us: gather_blocks(): got = lax.ppermute(block[None], axis, shift_pairs(count, step))]
    all_gather x2 -> x0, waiting for transfers between devices: 36.3 us -> none  [the longest x1 26.9 us: per_device(): whole = lax.all_gather(packed, 'row', axis=1, tiled=True)]
    add x2 -> x0, other arithmetic: 28.8 us -> none  [the longest x1 28.8 us: per_device(): alpha_all[None, :, None, :] * tiles]
    all_gather x2 -> x0, blocking collectives: 22.8 us -> none  [merge_stats(): every = lax.all_gather(stats, axis, axis=0, tiled=False)]
    unnamed x5 -> x0, other arithmetic: 19.2 us -> none
    dot_general x8 -> x0, matrix products: 16.8 us -> none  [the longest x6 7.34 us: project(): lax.dot_general(weight, normed, (((0,), (1,)), ((), ())), preferred_eleme...]
  transfers between devices with their start and end apart: 10 -> 0, of which waited for: 8 -> 0; matrix products, arithmetic and copies ran while one was open for 15% -> 0% of each run, Pallas kernels for 0% -> 0%
where the time goes in v1:
time: 184 us
  Pallas kernels  181 us (98%)
    pallas_call x1, Pallas kernels, fused_device(): pl.pallas_call(functools.partial(last_kernel, rows, cols, heads), out_sha...  109 us
    pallas_call x1, Pallas kernels, fused_device(): pl.pallas_call(functools.partial(first_kernel, rows, cols, heads, key_row...  29 us
    pallas_call x1, Pallas kernels, fused_device(): pl.pallas_call(functools.partial(update_kernel, heads, key_rows, tile), g...  26.1 us
    pallas_call x1, Pallas kernels, fused_device(): pl.pallas_call(functools.partial(response_kernel, heads, key_rows, tile,...  16.9 us

profile of v1, /device:TPU:0, one launch (start us, length us, event | category | flops | bytes accessed | tf_op | source)
XLA Modules:
  0.0 183.5 jit_solution(13882138297338626899)
XLA Ops:
  0.6 29.0 %first.1 = (bf16[4,288,128]{2,1,0:T(8,128)(2,1)}, f32[288,256]{1,0:T(8,128)}, f32[288,256]{1,0:T(8,128)}, f32[288,128]{1,0:T(8,128)}, f32[4,8,288]{2,1,0:T(8,128)}) custom-call(bf16[288,256]{1,0:T(8,128)(2,1)} %hid.3, bf16[2048]{0:T(1024)(128)(2,1)} %gain.1, bf16[2048,256]{1,0:T(8,128)(2,1)} %w4_hbm.1, bf16[2048,256]{1,0:T(8,128)(2,1)} %w5_hbm.1, ...), custom_call_target="tpu_custom_call" | custom-call | tf_op jit(solution)/shard_map/first/pallas_call | solution.py:677
  29.6 16.9 %responses.1 = (bf16[4,288,256]{2,1,0:T(8,128)(2,1)}, f32[4,288,256]{2,1,0:T(8,128)}, f32[64,1152]{1,0:T(8,128)}) custom-call(f32[32,256,1152]{2,1,0:T(8,128)} %state.3, bf16[1152,128]{1,0:T(8,128)(2,1)} %bitcast.7), custom_call_target="tpu_custom_call" | custom-call | tf_op jit(solution)/shard_map/responses/pallas_call | solution.py:704
  46.5 109.1 %last.1 = (bf16[4,288,256]{2,1,0:T(8,128)(2,1)}, f32[1152]{0:T(1024)}, f32[1152]{0:T(1024)}, f32[1152]{0:T(1024)}) custom-call(bf16[4,288,256]{2,1,0:T(8,128)(2,1)} %get-tuple-element.19.recalls, f32[4,288,256]{2,1,0:T(8,128)} %get-tuple-element.20.answers, f32[288,256]{1,0:T(8,128)} %get-tuple-element.21.value, f32[288,256]{1,0:T(8,128)} %get-tuple-element.22.gate, ...), custom_call_target="tpu_custom_call" | custom-call | tf_op jit(solution)/shard_map/last/pallas_call | solution.py:722
  155.6 0.0 copy-start.2
  155.6 0.0 copy-start.1
  155.6 0.0 copy-start
  155.6 26.1 %update.1 = f32[32,256,1152]{2,1,0:T(8,128)} custom-call(f32[32,256,1152]{2,1,0:T(8,128)} %state.3, f32[64,1152]{1,0:T(8,128)} %get-tuple-element.17.key, f32[4,8,288]{2,1,0:T(8,128)} %get-tuple-element.18.alpha, bf16[1152,256]{1,0:T(8,128)(2,1)} %bitcast.6), custom_call_target="tpu_custom_call" | custom-call | tf_op jit(solution)/shard_map/update/pallas_call | solution.py:752
  181.7 0.0 copy-done.2
  181.7 0.6 copy.24
  182.3 0.0 copy-done.1
  182.3 0.6 copy.25
  182.9 0.0 copy-done
  182.9 0.6 copy.26
Async XLA Ops:
  155.6 26.1 %copy-start.2 = (f32[1152]{0:T(1024)S(1)}, f32[1152]{0:T(1024)}, u32[]{:S(2)}) copy-start(f32[1152]{0:T(1024)} %get-tuple-element.33) | copy-start | bytes 13828
  155.6 26.7 %copy-start.1 = (f32[1152]{0:T(1024)S(1)}, f32[1152]{0:T(1024)}, u32[]{:S(2)}) copy-start(f32[1152]{0:T(1024)} %get-tuple-element.34) | copy-start | bytes 13828
  155.6 27.3 %copy-start = (f32[1152]{0:T(1024)S(1)}, f32[1152]{0:T(1024)}, u32[]{:S(2)}) copy-start(f32[1152]{0:T(1024)} %get-tuple-element.35) | copy-start | bytes 13828
